TPU v7x, 32 devices: a whole 2x2x4 slice. The times are simulated.
32 devices in a mesh: blk: 16 (over z, y, x), obs: 2 (over core).
Axes of the slice: x: 2, y: 2, z: 4, core: 2. Of those that a mesh axis runs over, the one named last changes fastest.
Arguments:
- populations: float32 [16, 19, 32, 1024], P('blk', None, 'obs'), may hold values from 0.011111111 to 0.533333333, as said below
- block_faces: int32 [16, 4], P('blk'), may hold values from 0 to 15, as said below
- block_edges: int32 [16, 4], P('blk'), may hold values from 0 to 15, as said below
- probe_cell: int32 [4096], P(('blk', 'obs')), may hold values from 0 to 16383
- history: bfloat16 [4096, 512], P(('blk', 'obs')), may hold values from -6 to 6
- panel_count: int32 [32], P(('blk', 'obs')), may hold values from 0 to 128, as said below
- panel_owner: int32 [4096], P(('blk', 'obs')), may hold values from 0 to 1023, as said below
- panel_pos: bfloat16 [3, 2048], P(None, ('blk', 'obs')), may hold values from -1 to 1
- panel_normal: bfloat16 [3, 2048], P(None, ('blk', 'obs')), may hold values from -0.625 to 0.625
- observers: float32 [3, 1024], P(None, 'obs'), may hold values from -8 to 8, as said below
Outputs:
- populations_out: float32 [16, 19, 32, 1024], P('blk', None, 'obs')
- spectrum: float32 [2, 512, 128], P('obs', 'blk')
Inputs may be any that keep to these rules, and one draw needn't show every extreme that they name: `populations`: every population is positive. The blocks form a lattice of 4 by 4 blocks along y and z, periodic in both, one block deep in x; block_faces[b] names the blocks beside b at -y, +y, -z, +z. block_edges[b] names the blocks at (-y,-z), (-y,+z), (+y,-z), (+y,+z) of b: the y neighbour's z neighbour, which is the z neighbour's y neighbour. The eight face and edge neighbours of a block are distinct and differ from it. The live slots of a device are its first panel_count slots. The counts of the devices at one obs index sum to 1024. `panel_owner`: in a live slot of the device at blk index b and obs index o the value is q * 64 + j: slot j of the owner at blk index q and the same obs index. Every owner slot receives exactly one live panel. A device sends at most 8 live panels to one owner, and its live panels go to the owners in numbers that differ by at most one. Dead slots hold arbitrary values of the range. `observers`: every observer lies at a distance of 4 to 8 from the anchor (0, 0, 0).
All inputs are finite; a program needn't handle non-finite values.
Results may differ from a plain program's by a relative error of at most 0.0032.
The roundings to bfloat16 on the way count: a program that leaves them out, or rounds other values in their place, can miss the bound.
Values may be sent and summed in bfloat16 or wider, within the bound.
A program may use at most 128 MiB of HBM per device.

v0:
```python
import math
import jax
import jax.numpy as jnp
from jax import lax
from jax.sharding import PartitionSpec as P

BS = 32
STEPS = 4
SAMPLES = 256
BINS = 64
P_OWN = 64
velocity_list = [
    (0, 0, 0),
    (1, 0, 0),
    (-1, 0, 0),
    (0, 1, 0),
    (0, -1, 0),
    (0, 0, 1),
    (0, 0, -1),
    (1, 1, 0),
    (-1, -1, 0),
    (1, -1, 0),
    (-1, 1, 0),
    (1, 0, 1),
    (-1, 0, -1),
    (1, 0, -1),
    (-1, 0, 1),
    (0, 1, 1),
    (0, -1, -1),
    (0, 1, -1),
    (0, -1, 1),
]
weight_list = [1.0 / 3.0] + [1.0 / 18.0] * 6 + [1.0 / 36.0] * 12
x_moving = [1, 2, 7, 8, 9, 10, 11, 12, 13, 14]
y_upward = [3, 7, 10, 15, 17]
y_downward = [4, 8, 9, 16, 18]
z_upward = [5, 11, 14, 15, 18]
z_downward = [6, 12, 13, 16, 17]
relax_rate = 1.6
pressure_gain = 60.0
sound_speed = 0.5


def padded(block, sides, width):
    for axis, dim in sides:
        count = lax.axis_size(axis)
        forward = [(i, i + 1) for i in range(count - 1)]
        forward.append((count - 1, 0))
        backward = [(target, source) for source, target in forward]
        low = lax.ppermute(
            lax.slice_in_dim(block, block.shape[dim] - width, None, axis=dim), axis, forward
        )
        high = lax.ppermute(lax.slice_in_dim(block, 0, width, axis=dim), axis, backward)
        block = jnp.concatenate([low, block, high], axis=dim)
    return block


def component(axis_number, extra):
    values = jnp.array([velocity[axis_number] for velocity in velocity_list], jnp.float32)
    return values.reshape((19,) + extra)


def collide(field):
    extra = (1,) * (field.ndim - 1)
    along_x = component(0, extra)
    along_y = component(1, extra)
    along_z = component(2, extra)
    weights = jnp.array(weight_list, jnp.float32).reshape((19,) + extra)
    density = jnp.sum(field, axis=0)
    speed_x = jnp.sum(along_x * field, axis=0) / density
    speed_y = jnp.sum(along_y * field, axis=0) / density
    speed_z = jnp.sum(along_z * field, axis=0) / density
    projected = along_x * speed_x + along_y * speed_y + along_z * speed_z
    squared = speed_x * speed_x + speed_y * speed_y + speed_z * speed_z
    equilibrium = (
        weights * density * (1.0 + 3.0 * projected + 4.5 * projected * projected - 1.5 * squared)
    )
    return field + relax_rate * (equilibrium - field)


def stream_merged(widened, planes):
    below_plane, above_plane, near_plane, far_plane = planes
    slab_depth = widened.shape[1] - 2
    lane_count = widened.shape[2]
    lane_index = jnp.arange(lane_count, dtype=jnp.int32)
    lane_row = lane_index // BS
    lane_column = lane_index % BS
    parts = []
    for number, velocity in enumerate(velocity_list):
        shift_x, shift_y, shift_z = velocity
        begin = 1 - shift_x
        moved = jnp.roll(
            widened[number, begin : begin + slab_depth], shift_y * BS + shift_z, axis=-1
        )
        if shift_y != 0:
            source_plane = below_plane if shift_y == 1 else above_plane
            row_values = jnp.roll(
                source_plane[number, begin : begin + slab_depth], shift_z, axis=-1
            )
            edge_index = 0 if shift_y == 1 else BS - 1
            moved = jnp.where(
                (lane_row == edge_index)[None, :], jnp.tile(row_values, (1, BS)), moved
            )
        if shift_z != 0:
            source_plane = near_plane if shift_z == 1 else far_plane
            column_values = source_plane[
                number, begin : begin + slab_depth, 1 - shift_y : 1 - shift_y + BS
            ]
            edge_index = 0 if shift_z == 1 else BS - 1
            moved = jnp.where(
                (lane_column == edge_index)[None, :], jnp.repeat(column_values, BS, axis=-1), moved
            )
        parts.append(moved)
    return jnp.stack(parts)


def place_pieces(pieces, targets, blocks):
    onehot = (targets[:, None] == jnp.arange(blocks, dtype=jnp.int32)[None, :]).astype(jnp.float32)
    return jnp.einsum("kn,kf->nf", onehot, pieces, precision=lax.Precision.HIGHEST)


def spread_pops(piece, chosen, shape):
    return jnp.zeros(shape, jnp.float32).at[jnp.array(chosen)].set(piece)


def direct_halo(widened, block_faces, block_edges, blocks):
    depth_x = widened.shape[1]
    lane_count = widened.shape[2]

    def corner_piece(number, lane_at):
        return jnp.zeros((5, depth_x, BS), jnp.float32).at[0, :, 0].set(widened[number, :, lane_at])

    def corner_plane(number, vector):
        return jnp.zeros((19, depth_x, 1), jnp.float32).at[number, :, 0].set(vector)

    outgoing = jnp.stack(
        [
            widened[jnp.array(y_downward), :, 0:BS],
            widened[jnp.array(y_upward), :, lane_count - BS :],
            widened[jnp.array(z_downward), :, 0::BS],
            widened[jnp.array(z_upward), :, BS - 1 :: BS],
            corner_piece(16, 0),
            corner_piece(18, BS - 1),
            corner_piece(17, (BS - 1) * BS),
            corner_piece(15, BS * BS - 1),
        ]
    ).reshape(8, -1)
    targets = jnp.concatenate([block_faces, block_edges])
    received = lax.all_to_all(
        place_pieces(outgoing, targets, blocks), "blk", split_axis=0, concat_axis=0, tiled=True
    )
    chosen = jnp.take(received, targets, axis=0).reshape(8, 5, depth_x, BS)
    below_plane = spread_pops(chosen[0], y_upward, (19, depth_x, BS))
    above_plane = spread_pops(chosen[1], y_downward, (19, depth_x, BS))
    near_core = spread_pops(chosen[2], z_upward, (19, depth_x, BS))
    far_core = spread_pops(chosen[3], z_downward, (19, depth_x, BS))
    near_plane = jnp.concatenate(
        [corner_plane(15, chosen[4, 0, :, 0]), near_core, corner_plane(18, chosen[6, 0, :, 0])],
        axis=2,
    )
    far_plane = jnp.concatenate(
        [corner_plane(17, chosen[5, 0, :, 0]), far_core, corner_plane(16, chosen[7, 0, :, 0])],
        axis=2,
    )
    return (below_plane, above_plane, near_plane, far_plane)


def transform_table():
    moments = jnp.arange(SAMPLES, dtype=jnp.int32)[:, None]
    harmonics = jnp.arange(BINS, dtype=jnp.int32)[None, :] + 1
    turns = moments * harmonics % SAMPLES
    phases = turns.astype(jnp.float32) * (2.0 * math.pi / SAMPLES)
    return jnp.concatenate([jnp.cos(phases), -jnp.sin(phases)], axis=1).astype(jnp.bfloat16)


def radiate(spectra, place, normal, listen):
    values = spectra.astype(jnp.float32)
    press_real = values[0:BINS].T
    press_imag = values[BINS : 2 * BINS].T
    rate_real = values[2 * BINS : 3 * BINS].T
    rate_imag = values[3 * BINS : 4 * BINS].T
    offsets = listen[:, None, :] - place.astype(jnp.float32)[:, :, None]
    distance_sq = jnp.sum(offsets * offsets, axis=0)
    distance = jnp.sqrt(distance_sq)
    facing = jnp.sum(normal.astype(jnp.float32)[:, :, None] * offsets, axis=0)
    far_term = facing / (4.0 * math.pi * sound_speed * distance_sq)
    near_term = facing / (4.0 * math.pi * distance_sq * distance)
    angular = (jnp.arange(BINS, dtype=jnp.float32) + 1.0) * (2.0 * math.pi / SAMPLES)
    phases = angular[None, :, None] * (distance / sound_speed)[:, None, :]
    cosine = jnp.cos(phases)
    sine_part = jnp.sin(phases)
    weight_real = (
        far_term[:, None, :] * rate_real[:, :, None]
        + near_term[:, None, :] * press_real[:, :, None]
    )
    weight_imag = (
        far_term[:, None, :] * rate_imag[:, :, None]
        + near_term[:, None, :] * press_imag[:, :, None]
    )
    real_part = jnp.sum(weight_real * cosine + weight_imag * sine_part, axis=0)
    imag_part = jnp.sum(weight_imag * cosine - weight_real * sine_part, axis=0)
    return jnp.concatenate([real_part, imag_part], axis=0).T


def radiate_blocks(spectra, place, normal, listen):
    count_panels = spectra.shape[1]
    listener_count = listen.shape[1]
    block_size = 128
    while block_size > 1 and (
        count_panels % block_size != 0 or block_size * listener_count > 16384
    ):
        block_size = block_size // 2

    def radiate_accumulate(block_number, total):
        begin = block_number * block_size
        return total + radiate(
            lax.dynamic_slice_in_dim(spectra, begin, block_size, 1),
            lax.dynamic_slice_in_dim(place, begin, block_size, 1),
            lax.dynamic_slice_in_dim(normal, begin, block_size, 1),
            listen,
        )

    return lax.fori_loop(
        0,
        count_panels // block_size,
        radiate_accumulate,
        jnp.zeros((listener_count, 2 * BINS), jnp.float32),
    )


def route_slots(payload, owners, alive_slot, blocks):
    count_slots = payload.shape[0]
    capacity = -(-count_slots // blocks)
    target = owners // P_OWN
    member = (
        (target[:, None] == jnp.arange(blocks, dtype=jnp.int32)[None, :]) & alive_slot[:, None]
    ).astype(jnp.int32)
    before = jnp.cumsum(member, axis=0) - member
    order_within = jnp.sum(before * member, axis=1)
    slot_label = jnp.where(alive_slot, target * capacity + order_within, -1)
    matches = slot_label[:, None] == jnp.arange(blocks * capacity, dtype=jnp.int32)[None, :]
    source = jnp.sum(
        jnp.where(matches, jnp.arange(count_slots, dtype=jnp.int32)[:, None], 0), axis=0
    )
    filled = jnp.any(matches, axis=0)
    outgoing = jnp.take(payload, source, axis=0).reshape(blocks, capacity, payload.shape[1])
    tagged = jnp.where(filled, jnp.take(owners, source), -1).reshape(blocks, capacity)
    return (outgoing, tagged)


def settle(incoming, tagged):
    keeper = lax.axis_index("blk")
    flat_tags = tagged.reshape(-1)
    slot_here = flat_tags - keeper * P_OWN
    choose = (
        (slot_here[:, None] == jnp.arange(P_OWN, dtype=jnp.int32)[None, :])
        & (flat_tags[:, None] >= 0)
    ).astype(jnp.bfloat16)
    return jnp.einsum(
        "rw,rp->wp",
        incoming.reshape(-1, incoming.shape[-1]),
        choose,
        preferred_element_type=jnp.float32,
    ).astype(jnp.bfloat16)


def body(
    populations,
    block_faces,
    block_edges,
    probe_cell,
    history,
    panel_count,
    panel_owner,
    panel_pos,
    panel_normal,
    observers,
):
    blocks = lax.axis_size("blk")
    lattice_state = populations[0]
    slab_depth = lattice_state.shape[1]
    lane_count = lattice_state.shape[2]
    faces_here = block_faces[0]
    edges_here = block_edges[0]
    readings = []
    for turn_index in range(STEPS):
        collided = collide(lattice_state)
        slab_edges = padded(collided[jnp.array(x_moving)], (("obs", 1),), 1)
        lower_plane = spread_pops(slab_edges[:, 0:1], x_moving, (19, 1, lane_count))
        upper_plane = spread_pops(slab_edges[:, -1:], x_moving, (19, 1, lane_count))
        widened = jnp.concatenate([lower_plane, collided, upper_plane], axis=1)
        planes = direct_halo(widened, faces_here, edges_here, blocks)
        lattice_state = stream_merged(widened, planes)
        density = jnp.sum(lattice_state, axis=0).reshape(-1)
        readings.append(jnp.take(density, probe_cell))
    populations_out = lattice_state.reshape(1, 19, slab_depth, lane_count)
    gained = pressure_gain * (jnp.stack(readings, axis=1) - 1.0)
    previous = jnp.concatenate(
        [history[:, SAMPLES - 1 : SAMPLES].astype(jnp.float32), gained[:, :-1]], axis=1
    )
    rate_values = gained - previous
    recent = jnp.concatenate(
        [
            history[:, STEPS:SAMPLES],
            gained.astype(jnp.bfloat16),
            history[:, SAMPLES + STEPS :],
            rate_values.astype(jnp.bfloat16),
        ],
        axis=1,
    )
    transform = transform_table()
    count_slots = recent.shape[0]
    alive_slot = jnp.arange(count_slots, dtype=jnp.int32) < panel_count[0]
    outgoing, tagged = route_slots(recent, panel_owner, alive_slot, blocks)
    incoming, tags_in = (
        lax.all_to_all(outgoing, "blk", split_axis=0, concat_axis=0, tiled=True),
        lax.all_to_all(tagged, "blk", split_axis=0, concat_axis=0, tiled=True),
    )
    histories = settle(incoming, tags_in).reshape(2, SAMPLES, P_OWN)
    spectra = (
        jnp.einsum("tk,gtp->gkp", transform, histories, preferred_element_type=jnp.float32)
        .astype(jnp.bfloat16)
        .reshape(4 * BINS, P_OWN)
    )
    partial_value = radiate_blocks(
        lax.all_gather(spectra, "obs", axis=1, tiled=True),
        lax.all_gather(panel_pos, "obs", axis=1, tiled=True),
        lax.all_gather(panel_normal, "obs", axis=1, tiled=True),
        observers,
    )
    summed = lax.psum_scatter(partial_value, "blk", scatter_dimension=0, tiled=True)
    return (populations_out, summed.reshape(1, -1, 2 * BINS))


def solution(mesh):
    placed = (
        P("blk", None, "obs", None),
        P("blk", None),
        P("blk", None),
        P(("blk", "obs")),
        P(("blk", "obs"), None),
        P(("blk", "obs")),
        P(("blk", "obs")),
        P(None, ("blk", "obs")),
        P(None, ("blk", "obs")),
        P(None, "obs"),
    )
    return jax.shard_map(
        body,
        mesh=mesh,
        in_specs=placed,
        out_specs=(P("blk", None, "obs", None), P("obs", "blk", None)),
        check_vma=False,
    )
```

profile of v0, /device:TPU:0, one launch (start us, length us, event | category | flops | bytes accessed | tf_op | source)
XLA Modules:
  0.0 673.8 jit_solution(10351201009113472713)
XLA Ops:
  21.0 1.9 all-gather.1
  56.1 5.3 copy.672
  61.4 7.4 %copy.668 = f32[19,18,1024]{1,0,2:T(8,128)} copy(f32[19,18,1024]{2,1,0:T(8,128)S(1)} %pad_maximum_fusion) | data formatting | bytes 2801664 | tf_op jit(solution)/shard_map/concatenate | solution.py:291
  69.6 2.7 gather_fusion.4
  72.3 2.7 gather_fusion.3
  80.6 8.4 %all-to-all-start = ((f32[16,1,2880]{2,1,0:T(1,128)}), f32[16,1,2880]{2,1,0:T(1,128)S(1)}, u32[]{:S(2)}, u32[]{:S(2)}) async-start(f32[16,1,2880]{2,1,0:T(1,128)} %copy.680), calls=%async_computation | async-start | bytes 376832 | tf_op jit(solution)/shard_map/all_to_all | solution.py:149
  184.0 5.2 copy.695
  189.2 3.4 gather_fusion.9
  192.6 3.4 gather_fusion.8
  196.0 7.4 %copy.691 = f32[19,18,1024]{1,0,2:T(8,128)} copy(f32[19,18,1024]{2,1,0:T(8,128)S(1)} %pad_maximum_fusion.1) | data formatting | bytes 2801664 | tf_op jit(solution)/shard_map/concatenate | solution.py:291
  209.7 7.3 %all-to-all-start.1 = ((f32[16,1,2880]{2,1,0:T(1,128)}), f32[16,1,2880]{2,1,0:T(1,128)S(1)}, u32[]{:S(2)}, u32[]{:S(2)}) async-start(f32[16,1,2880]{2,1,0:T(1,128)} %copy.703), calls=%async_computation.1 | async-start | bytes 376832 | tf_op jit(solution)/shard_map/all_to_all | solution.py:149
  312.2 5.2 copy.718
  317.4 3.4 gather_fusion.14
  320.8 3.4 gather_fusion.13
  324.2 7.4 %copy.714 = f32[19,18,1024]{1,0,2:T(8,128)} copy(f32[19,18,1024]{2,1,0:T(8,128)S(1)} %pad_maximum_fusion.2) | data formatting | bytes 2801664 | tf_op jit(solution)/shard_map/concatenate | solution.py:291
  337.9 7.1 %all-to-all-start.2 = ((f32[16,1,2880]{2,1,0:T(1,128)}), f32[16,1,2880]{2,1,0:T(1,128)S(1)}, u32[]{:S(2)}, u32[]{:S(2)}) async-start(f32[16,1,2880]{2,1,0:T(1,128)} %copy.726), calls=%async_computation.2 | async-start | bytes 376832 | tf_op jit(solution)/shard_map/all_to_all | solution.py:149
  429.7 5.2 copy.741
  434.9 2.7 gather_fusion.19
  437.7 2.7 gather_fusion.18
  440.4 7.4 %copy.737 = f32[19,18,1024]{1,0,2:T(8,128)} copy(f32[19,18,1024]{2,1,0:T(8,128)S(1)} %pad_maximum_fusion.3) | data formatting | bytes 2801664 | tf_op jit(solution)/shard_map/concatenate | solution.py:291
  453.9 6.9 %all-to-all-start.3 = ((f32[16,1,2880]{2,1,0:T(1,128)}), f32[16,1,2880]{2,1,0:T(1,128)S(1)}, u32[]{:S(2)}, u32[]{:S(2)}) async-start(f32[16,1,2880]{2,1,0:T(1,128)} %copy.749), calls=%async_computation.3 | async-start | bytes 376832 | tf_op jit(solution)/shard_map/all_to_all | solution.py:149
  463.5 5.7 all-to-all-done.3
  469.3 4.1 all-to-all-start.5
  505.0 7.0 %all-to-all-start.4 = ((bf16[16,8,512]{2,1,0:T(8,128)(2,1)}), bf16[16,8,512]{2,1,0:T(8,128)(2,1)S(1)}, u32[]{:S(2)}, u32[]{:S(2)}) async-start(bf16[16,8,512]{2,1,0:T(8,128)(2,1)} %bitcast_select_fusion), calls=%async_computation.4 | async-start | bytes 262144 | tf_op jit(solution)/shard_map/all_to_all | solution.py:316
  512.3 7.5 %all-to-all-done.4 = bf16[16,8,512]{2,1,0:T(8,128)(2,1)S(1)} async-done(((bf16[16,8,512]{2,1,0:T(8,128)(2,1)}), bf16[16,8,512]{2,1,0:T(8,128)(2,1)S(1)}, u32[]{:S(2)}, u32[]{:S(2)}) %all-to-all-start.4) | async-done | bytes 131104 | tf_op jit(solution)/shard_map/all_to_all | solution.py:316
  520.3 2.0 all_gather.11
  522.3 69.2 %while.46 = (s32[]{:T(128)}, f32[512,128]{0,1:T(8,128)S(1)}, bf16[3,128]{1,0:T(4,128)(2,1)S(1)}, f32[3,512]{1,0:T(4,128)S(1)}, bf16[3,128]{1,0:T(4,128)(2,1)S(1)...) while((s32[]{:T(128)}, f32[512,128]{0,1:T(8,128)S(1)}, ...), condition=%wide.region_46.49_spmd.clone, body=%wide.region_41.48_spmd.clone.sunk | while | flops 16179527 | bytes 1860141 | solution.py:223
  522.7 16.8 %fusion.295 = (f32[64,512]{1,0:T(8,128)S(1)}, f32[64,512]{1,0:T(8,128)S(1)}) fusion(f32[32,64]{1,0:T(8,128)S(1)} %get-tuple-element.1175, f32[32,64]{1,0:T(8,128)S(1)} %get-tuple-element.1176, f32[32,512]{1,0:T(8,128)S(1)} %get-tuple-element.1181, f32[64]{0:T(128)S(1)} %add_multiply_fusion.3, f32[32,64]{1,0:T(8,128)S(1)} %get-tuple-element.1182, ...), kind=kLoop, calls=%fused_computation.61.clone.1 | loop fusion | flops 15663104 | bytes 491776 | tf_op jit(solution)/shard_map/while/body/eval_jaxpr/reduce_sum | solution.py:200
  540.0 16.8 %fusion.295 = (f32[64,512]{1,0:T(8,128)S(1)}, f32[64,512]{1,0:T(8,128)S(1)}) fusion(f32[32,64]{1,0:T(8,128)S(1)} %get-tuple-element.1175, f32[32,64]{1,0:T(8,128)S(1)} %get-tuple-element.1176, f32[32,512]{1,0:T(8,128)S(1)} %get-tuple-element.1181, f32[64]{0:T(128)S(1)} %add_multiply_fusion.3, f32[32,64]{1,0:T(8,128)S(1)} %get-tuple-element.1182, ...), kind=kLoop, calls=%fused_computation.61.clone.1 | loop fusion | flops 15663104 | bytes 491776 | tf_op jit(solution)/shard_map/while/body/eval_jaxpr/reduce_sum | solution.py:200
  557.3 16.8 %fusion.295 = (f32[64,512]{1,0:T(8,128)S(1)}, f32[64,512]{1,0:T(8,128)S(1)}) fusion(f32[32,64]{1,0:T(8,128)S(1)} %get-tuple-element.1175, f32[32,64]{1,0:T(8,128)S(1)} %get-tuple-element.1176, f32[32,512]{1,0:T(8,128)S(1)} %get-tuple-element.1181, f32[64]{0:T(128)S(1)} %add_multiply_fusion.3, f32[32,64]{1,0:T(8,128)S(1)} %get-tuple-element.1182, ...), kind=kLoop, calls=%fused_computation.61.clone.1 | loop fusion | flops 15663104 | bytes 491776 | tf_op jit(solution)/shard_map/while/body/eval_jaxpr/reduce_sum | solution.py:200
  574.6 16.8 %fusion.295 = (f32[64,512]{1,0:T(8,128)S(1)}, f32[64,512]{1,0:T(8,128)S(1)}) fusion(f32[32,64]{1,0:T(8,128)S(1)} %get-tuple-element.1175, f32[32,64]{1,0:T(8,128)S(1)} %get-tuple-element.1176, f32[32,512]{1,0:T(8,128)S(1)} %get-tuple-element.1181, f32[64]{0:T(128)S(1)} %add_multiply_fusion.3, f32[32,64]{1,0:T(8,128)S(1)} %get-tuple-element.1182, ...), kind=kLoop, calls=%fused_computation.61.clone.1 | loop fusion | flops 15663104 | bytes 491776 | tf_op jit(solution)/shard_map/while/body/eval_jaxpr/reduce_sum | solution.py:200
  592.4 74.4 %reduce-scatter.2.cloned.1.call-done = f32[32,128]{1,0:T(8,128)} async-done(((f32[512,128]{1,0:T(8,128)}), f32[32,128]{1,0:T(8,128)}) %reduce-scatter.2.cloned.1.call-update) | async-done | bytes 16400 | tf_op jit(solution)/shard_map/reduce_scatter | solution.py:331
  (1816 shorter events, 376.1 us)
Async XLA Ops:
  11.5 11.5 %copy-start.426 = (bf16[3,64]{1,0:T(4,128)(2,1)S(1)}, bf16[3,64]{1,0:T(4,128)(2,1)}, u32[]{:S(2)}) copy-start(bf16[3,64]{1,0:T(4,128)(2,1)} %param.148) | copy-start | bytes 1156
  12.2 19.8 %collective-permute-start = (f32[10,1,1024]{2,1,0:T(1,128)S(1)}, f32[10,1,1024]{2,1,0:T(1,128)S(1)}, u32[]{:S(2)}, u32[]{:S(2)}) collective-permute-start(f32[10,1,1024]{2,1,0:T(1,128)S(1)} %get-tuple-element.752), channel_id=1, source_target_pairs={{0,1},{1,0},{2,3},{3,2},{4,5},{5,4},{6,7},{7,6},{8,9},{9,8},{10,11... | collective-permute-start | bytes 122888 | tf_op jit(solution)/shard_map/ppermute | solution.py:50
  12.7 18.4 %collective-permute-start.1 = (f32[10,1,1024]{2,1,0:T(1,128)S(1)}, f32[10,1,1024]{2,1,0:T(1,128)S(1)}, u32[]{:S(2)}, u32[]{:S(2)}) collective-permute-start(f32[10,1,1024]{2,1,0:T(1,128)S(1)} %get-tuple-element.753), channel_id=1, source_target_pairs={{1,0},{0,1},{3,2},{2,3},{5,4},{4,5},{7,6},{6,7},{9,8},{8,9},{11,10... | collective-permute-start | bytes 122888 | tf_op jit(solution)/shard_map/ppermute | solution.py:53
  16.8 14.2 %copy-start.420 = (s32[1024]{0:T(1024)}, s32[1024]{0:T(1024)S(1)}, u32[]{:S(2)}) copy-start(s32[1024]{0:T(1024)S(1)} %get-tuple-element.1095) | copy-start | bytes 12292
  77.0 12.0 %copy-start.161 = (f32[16,992]{1,0:T(8,128)S(1)}, f32[16,992]{1,0:T(8,128)}, u32[]{:S(2)}) copy-start(f32[16,992]{1,0:T(8,128)} %get-tuple-element.1039) | copy-start | bytes 190468
  77.0 12.0 %copy-start.320 = (f32[16,32]{1,0:T(8,128)S(1)}, f32[16,32]{1,0:T(8,128)}, u32[]{:S(2)}) copy-start(f32[16,32]{1,0:T(8,128)} %get-tuple-element.1037) | copy-start | bytes 6148
  77.0 12.1 %copy-start.164 = (f32[16,992]{1,0:T(8,128)S(1)}, f32[16,992]{1,0:T(8,128)}, u32[]{:S(2)}) copy-start(f32[16,992]{1,0:T(8,128)} %get-tuple-element.1045) | copy-start | bytes 190468
  77.0 12.1 %copy-start.323 = (f32[16,32]{1,0:T(8,128)S(1)}, f32[16,32]{1,0:T(8,128)}, u32[]{:S(2)}) copy-start(f32[16,32]{1,0:T(8,128)} %get-tuple-element.1047) | copy-start | bytes 6148
  77.0 12.1 %copy-start.167 = (f32[16,1023]{1,0:T(8,128)S(1)}, f32[16,1023]{1,0:T(8,128)}, u32[]{:S(2)}) copy-start(f32[16,1023]{1,0:T(8,128)} %get-tuple-element.1055) | copy-start | bytes 196420
  77.0 12.1 %copy-start.326 = (f32[16,1]{1,0:T(8,128)S(1)}, f32[16,1]{1,0:T(8,128)}, u32[]{:S(2)}) copy-start(f32[16,1]{1,0:T(8,128)} %get-tuple-element.1053) | copy-start | bytes 196
  77.0 12.2 %copy-start.170 = (f32[16,992]{1,0:T(8,128)S(1)}, f32[16,992]{1,0:T(8,128)}, u32[]{:S(2)}) copy-start(f32[16,992]{1,0:T(8,128)} %get-tuple-element.1041) | copy-start | bytes 190468
  77.1 12.2 %copy-start.329 = (f32[16,32]{1,0:T(8,128)S(1)}, f32[16,32]{1,0:T(8,128)}, u32[]{:S(2)}) copy-start(f32[16,32]{1,0:T(8,128)} %get-tuple-element.1043) | copy-start | bytes 6148
  80.6 20.7 %all-to-all-start = ((f32[16,1,2880]{2,1,0:T(1,128)}), f32[16,1,2880]{2,1,0:T(1,128)S(1)}, u32[]{:S(2)}, u32[]{:S(2)}) async-start(f32[16,1,2880]{2,1,0:T(1,128)} %copy.680), calls=%async_computation | async-start | bytes 376832 | tf_op jit(solution)/shard_map/all_to_all | solution.py:149
  154.7 5.0 collective-permute-start.2
  154.7 4.1 collective-permute-start.3
  209.7 19.7 %all-to-all-start.1 = ((f32[16,1,2880]{2,1,0:T(1,128)}), f32[16,1,2880]{2,1,0:T(1,128)S(1)}, u32[]{:S(2)}, u32[]{:S(2)}) async-start(f32[16,1,2880]{2,1,0:T(1,128)} %copy.703), calls=%async_computation.1 | async-start | bytes 376832 | tf_op jit(solution)/shard_map/all_to_all | solution.py:149
  218.4 11.0 %copy-start.3 = (f32[19,16,1024]{2,1,0:T(8,128)S(1)}, f32[19,16,1024]{2,1,0:T(8,128)}, u32[]{:S(2)}) copy-start(f32[19,16,1024]{2,1,0:T(8,128)} %get-tuple-element.735) | copy-start | bytes 3735556
  282.9 4.9 collective-permute-start.4
  282.9 4.1 collective-permute-start.5
  337.9 19.5 %all-to-all-start.2 = ((f32[16,1,2880]{2,1,0:T(1,128)}), f32[16,1,2880]{2,1,0:T(1,128)S(1)}, u32[]{:S(2)}, u32[]{:S(2)}) async-start(f32[16,1,2880]{2,1,0:T(1,128)} %copy.726), calls=%async_computation.2 | async-start | bytes 376832 | tf_op jit(solution)/shard_map/all_to_all | solution.py:149
  410.9 5.0 collective-permute-start.6
  410.9 4.1 collective-permute-start.7
  453.9 20.2 %copy-start.404 = (pred[8]{0:T(512)(128)(4,1)S(1)}, pred[8]{0:T(512)(128)(4,1)}, u32[]{:S(2)}) copy-start(pred[8]{0:T(512)(128)(4,1)} %get-tuple-element.651) | copy-start | bytes 28
  453.9 15.4 %all-to-all-start.3 = ((f32[16,1,2880]{2,1,0:T(1,128)}), f32[16,1,2880]{2,1,0:T(1,128)S(1)}, u32[]{:S(2)}, u32[]{:S(2)}) async-start(f32[16,1,2880]{2,1,0:T(1,128)} %copy.749), calls=%async_computation.3 | async-start | bytes 376832 | tf_op jit(solution)/shard_map/all_to_all | solution.py:149
  461.5 12.9 %copy-start.414 = (s32[5]{0:T(128)S(1)}, s32[5]{0:T(128)}, u32[]{:S(2)}) copy-start(s32[5]{0:T(128)} %constant.1290) | copy-start | bytes 64
  469.3 35.7 %all-to-all-start.5 = ((s32[16,1,8]{2,1,0:T(1,128)}), s32[16,1,8]{2,1,0:T(1,128)S(1)}, u32[]{:S(2)}, u32[]{:S(2)}) async-start(s32[16,1,8]{2,1,0:T(1,128)} %bitcast.352), calls=%async_computation.5 | async-start | bytes 16384 | tf_op jit(solution)/shard_map/all_to_all | solution.py:317
  502.8 17.4 %copy-start.370 = (bf16[256,64]{0,1:T(8,128)(2,1)S(1)}, bf16[256,64]{0,1:T(8,128)(2,1)}, u32[]{:S(2)}) copy-start(bf16[256,64]{0,1:T(8,128)(2,1)} %get-tuple-element.1085) | copy-start | bytes 98308
  502.8 17.3 %copy-start.371 = (bf16[256,64]{0,1:T(8,128)(2,1)S(1)}, bf16[256,64]{0,1:T(8,128)(2,1)}, u32[]{:S(2)}) copy-start(bf16[256,64]{0,1:T(8,128)(2,1)} %get-tuple-element.1086) | copy-start | bytes 98308
  503.2 19.2 %copy-start.265 = (f32[3,512]{1,0:T(4,128)S(1)}, f32[3,512]{1,0:T(4,128)}, u32[]{:S(2)}) copy-start(f32[3,512]{1,0:T(4,128)} %param.149) | copy-start | bytes 18436
  503.2 19.2 %copy-start.307 = (bf16[128,3]{0,1:T(4,128)(2,1)S(1)}, bf16[128,3]{0,1:T(4,128)(2,1)}, u32[]{:S(2)}) copy-start(bf16[128,3]{0,1:T(4,128)(2,1)} %reshape.9282) | copy-start | bytes 2308
  505.0 14.8 %all-to-all-start.4 = ((bf16[16,8,512]{2,1,0:T(8,128)(2,1)}), bf16[16,8,512]{2,1,0:T(8,128)(2,1)S(1)}, u32[]{:S(2)}, u32[]{:S(2)}) async-start(bf16[16,8,512]{2,1,0:T(8,128)(2,1)} %bitcast_select_fusion), calls=%async_computation.4 | async-start | bytes 262144 | tf_op jit(solution)/shard_map/all_to_all | solution.py:316
  512.0 154.8 %reduce-scatter.2.cloned.1.call-start = ((), (), s32[]{:S(2)}) async-start(), calls=%async_computation.7 | async-start | bytes 278528 | tf_op jit(solution)/shard_map/reduce_scatter | solution.py:331
  (415 other events, 2445.9 us)
Sparse Core Ops, SparseCore 0:
  592.5 74.2 reduce-scatter.1
where the time goes:
time: 686 us; the launch traced here: 674 us
  local copies, waits for them, and re-layouts  360 us (52%)
  other arithmetic  153 us (22%)
  waiting for transfers between devices  87.7 us (13%)
  starting transfers between devices  43.1 us (6%)
  between operations  22.8 us (3%)
    reduce_scatter x1, waiting for transfers between devices, body(): lax.psum_scatter(partial_value, 'blk', scatter_dimension=0, tiled=True)  74.4 us
    reduce_sum x4, other arithmetic, radiate(): real_part = jnp.sum(weight_real * cosine + weight_imag * sine_part, axis=0)  67.3 us
    slice x96, local copies, waits for them, and re-layouts, stream_merged(): jnp.roll(widened[number, begin:begin + slab_depth], shift_y * BS + shift_...  63.9 us
    unnamed x110, other arithmetic  53.2 us
    concatenate x8, local copies, waits for them, and re-layouts, body(): widened = jnp.concatenate([lower_plane, collided, upper_plane], axis=1)  50.4 us
    another operation x120, local copies, waits for them, and re-layouts, stream_merged(): jnp.tile(row_values, (1, BS))  48.2 us
    reshape x80, local copies, waits for them, and re-layouts, stream_merged(): jnp.repeat(column_values, BS, axis=-1)  47.6 us
    unnamed x979, local copies, waits for them, and re-layouts  44.4 us
  transfers between devices with their start and end apart: 15, of which 3 were waited for; matrix products, arithmetic and copies ran while one was open for 14% of the time, Pallas kernels for 0%

commit v1 on v0

--- a/solution.py
+++ b/solution.py
@@ -41,6 +41,18 @@
 sound_speed = 0.5
 
 
+def in_blocks(x, dim, size):
+    dims = x.shape
+    blocks = x.reshape(*dims[:dim], size, dims[dim] // size, *dims[dim + 1 :])
+    return jnp.moveaxis(blocks, dim, 0)
+
+
+def in_order(blocks, dim):
+    blocks = jnp.moveaxis(blocks, 0, dim)
+    dims = blocks.shape
+    return blocks.reshape(*dims[:dim], dims[dim] * dims[dim + 1], *dims[dim + 2 :])
+
+
 def padded(block, sides, width):
     for axis, dim in sides:
         count = lax.axis_size(axis)
@@ -146,9 +158,17 @@
         ]
     ).reshape(8, -1)
     targets = jnp.concatenate([block_faces, block_edges])
-    received = lax.all_to_all(
-        place_pieces(outgoing, targets, blocks), "blk", split_axis=0, concat_axis=0, tiled=True
-    )
+    x = place_pieces(outgoing, targets, blocks)
+    count_2, place_2 = (lax.axis_size("blk"), lax.axis_index("blk"))
+    tiles = in_blocks(x, 0, count_2)
+    done = [tiles[place_2]]
+    for lap in range(1, count_2):
+        sent = tiles[(place_2 + lap) % count_2]
+        done.append(
+            lax.ppermute(sent, "blk", [(i_2, (i_2 + lap) % count_2) for i_2 in range(count_2)])
+        )
+    tiles = jnp.stack(done)[(place_2 - jnp.arange(count_2)) % count_2]
+    received = in_order(tiles, 0)
     chosen = jnp.take(received, targets, axis=0).reshape(8, 5, depth_x, BS)
     below_plane = spread_pops(chosen[0], y_upward, (19, depth_x, BS))
     above_plane = spread_pops(chosen[1], y_downward, (19, depth_x, BS))

time: 686 us -> 816 us (1.19)
  starting transfers between devices: 43.1 us -> 125 us
  other arithmetic: 153 us -> 179 us
  local copies, waits for them, and re-layouts: 360 us -> 380 us
    ppermute x0 -> x60, starting transfers between devices: none -> 111 us  [direct_halo(): lax.ppermute(sent, 'blk', [(i_2, (i_2 + lap) % count_2) for i_2 in range(...]
    all_to_all x4 -> x0, starting transfers between devices: 29.8 us -> none  [direct_halo(): lax.all_to_all(place_pieces(outgoing, targets, blocks), 'blk', split_axis...]
    unnamed x110, other arithmetic: 53.2 us -> 77.5 us
    another operation x20 -> x24, local copies, waits for them, and re-layouts: 0.3 us -> 8.49 us  [the longest x4 5.91 us: direct_halo(): tiles = jnp.stack(done)[(place_2 - jnp.arange(count_2)) % count_2]]
    unnamed x979 -> x947, local copies, waits for them, and re-layouts: 44.4 us -> 46.3 us
  transfers between devices with their start and end apart: 15 -> 71, of which waited for: 3 -> 5; matrix products, arithmetic and copies ran while one was open for 14% -> 60% of each run, Pallas kernels for 0% -> 0%
where the time goes in v1:
time: 816 us; the launch traced here: 802 us
  local copies, waits for them, and re-layouts  380 us (47%)
  other arithmetic  179 us (22%)
  starting transfers between devices  125 us (15%)
  waiting for transfers between devices  87.2 us (11%)
  between operations  22.8 us (3%)
    ppermute x60, starting transfers between devices, direct_halo(): lax.ppermute(sent, 'blk', [(i_2, (i_2 + lap) % count_2) for i_2 in range(...  111 us
    unnamed x110, other arithmetic  77.5 us
    reduce_scatter x1, waiting for transfers between devices, body(): lax.psum_scatter(partial_value, 'blk', scatter_dimension=0, tiled=True)  74.4 us
    reduce_sum x4, other arithmetic, radiate(): real_part = jnp.sum(weight_real * cosine + weight_imag * sine_part, axis=0)  67.3 us
    slice x96, local copies, waits for them, and re-layouts, stream_merged(): jnp.roll(widened[number, begin:begin + slab_depth], shift_y * BS + shift_...  64 us
    concatenate x8, local copies, waits for them, and re-layouts, body(): widened = jnp.concatenate([lower_plane, collided, upper_plane], axis=1)  50.6 us
    another operation x120, local copies, waits for them, and re-layouts, stream_merged(): jnp.tile(row_values, (1, BS))  48.1 us
    reshape x80, local copies, waits for them, and re-layouts, stream_merged(): jnp.repeat(column_values, BS, axis=-1)  47.6 us
  transfers between devices with their start and end apart: 71, of which 5 were waited for; matrix products, arithmetic and copies ran while one was open for 60% of the time, Pallas kernels for 0%

profile of v1, /device:TPU:0, one launch (start us, length us, event | category | flops | bytes accessed | tf_op | source)
XLA Modules:
  0.0 802.2 jit_solution(17869407739319661460)
XLA Ops:
  12.4 8.4 %all-to-all-start.1 = ((s32[16,1,8]{2,1,0:T(1,128)}), s32[16,1,8]{2,1,0:T(1,128)}, u32[]{:S(2)}, u32[]{:S(2)}) async-start(s32[16,1,8]{2,1,0:T(1,128)} %bitcast.417), calls=%async_computation.1 | async-start | bytes 16384 | tf_op jit(solution)/shard_map/all_to_all | solution.py:337
  66.6 5.2 copy.660
  71.8 7.4 copy.656
  91.8 5.5 collective-permute-start.16
  110.0 4.1 collective-permute-start.11
  226.7 5.2 copy.682
  231.9 3.3 gather_fusion.10
  235.2 3.3 gather_fusion.9
  238.5 7.4 copy.678
  254.4 5.7 collective-permute-start.33
  273.3 3.8 collective-permute-start.28
  278.7 3.7 collective-permute-start.25
  391.2 5.2 copy.704
  396.4 3.3 gather_fusion.16
  403.0 7.4 copy.700
  418.9 5.7 collective-permute-start.50
  436.6 4.1 collective-permute-start.45
  543.9 5.2 copy.726
  554.4 7.5 copy.722
  567.4 5.7 collective-permute-start.67
  577.2 3.8 collective-permute-start.62
  582.6 3.8 collective-permute-start.59
  590.4 3.4 collective-permute-start.55
  600.1 4.0 collective-permute-done.53
  636.9 3.5 all-to-all-start
  642.1 6.1 all-to-all-done
  650.8 69.2 %while.46 = (s32[]{:T(128)}, f32[512,128]{0,1:T(8,128)S(1)}, bf16[3,128]{1,0:T(4,128)(2,1)S(1)}, f32[3,512]{1,0:T(4,128)S(1)}, bf16[3,128]{1,0:T(4,128)(2,1)S(1)...) while((s32[]{:T(128)}, f32[512,128]{0,1:T(8,128)S(1)}, ...), condition=%wide.region_46.49_spmd.clone, body=%wide.region_41.48_spmd.clone.sunk | while | flops 16179527 | bytes 1860141 | solution.py:243
  651.1 16.8 %fusion.305 = (f32[64,512]{1,0:T(8,128)S(1)}, f32[64,512]{1,0:T(8,128)S(1)}) fusion(f32[32,64]{1,0:T(8,128)S(1)} %get-tuple-element.1239, f32[32,64]{1,0:T(8,128)S(1)} %get-tuple-element.1240, f32[32,512]{1,0:T(8,128)S(1)} %get-tuple-element.1245, f32[64]{0:T(128)S(1)} %add_multiply_fusion.3, f32[32,64]{1,0:T(8,128)S(1)} %get-tuple-element.1246, ...), kind=kLoop, calls=%fused_computation.65.clone.1 | loop fusion | flops 15663104 | bytes 491776 | tf_op jit(solution)/shard_map/while/body/eval_jaxpr/reduce_sum | solution.py:220
  668.4 16.8 %fusion.305 = (f32[64,512]{1,0:T(8,128)S(1)}, f32[64,512]{1,0:T(8,128)S(1)}) fusion(f32[32,64]{1,0:T(8,128)S(1)} %get-tuple-element.1239, f32[32,64]{1,0:T(8,128)S(1)} %get-tuple-element.1240, f32[32,512]{1,0:T(8,128)S(1)} %get-tuple-element.1245, f32[64]{0:T(128)S(1)} %add_multiply_fusion.3, f32[32,64]{1,0:T(8,128)S(1)} %get-tuple-element.1246, ...), kind=kLoop, calls=%fused_computation.65.clone.1 | loop fusion | flops 15663104 | bytes 491776 | tf_op jit(solution)/shard_map/while/body/eval_jaxpr/reduce_sum | solution.py:220
  685.7 16.8 %fusion.305 = (f32[64,512]{1,0:T(8,128)S(1)}, f32[64,512]{1,0:T(8,128)S(1)}) fusion(f32[32,64]{1,0:T(8,128)S(1)} %get-tuple-element.1239, f32[32,64]{1,0:T(8,128)S(1)} %get-tuple-element.1240, f32[32,512]{1,0:T(8,128)S(1)} %get-tuple-element.1245, f32[64]{0:T(128)S(1)} %add_multiply_fusion.3, f32[32,64]{1,0:T(8,128)S(1)} %get-tuple-element.1246, ...), kind=kLoop, calls=%fused_computation.65.clone.1 | loop fusion | flops 15663104 | bytes 491776 | tf_op jit(solution)/shard_map/while/body/eval_jaxpr/reduce_sum | solution.py:220
  703.0 16.8 %fusion.305 = (f32[64,512]{1,0:T(8,128)S(1)}, f32[64,512]{1,0:T(8,128)S(1)}) fusion(f32[32,64]{1,0:T(8,128)S(1)} %get-tuple-element.1239, f32[32,64]{1,0:T(8,128)S(1)} %get-tuple-element.1240, f32[32,512]{1,0:T(8,128)S(1)} %get-tuple-element.1245, f32[64]{0:T(128)S(1)} %add_multiply_fusion.3, f32[32,64]{1,0:T(8,128)S(1)} %get-tuple-element.1246, ...), kind=kLoop, calls=%fused_computation.65.clone.1 | loop fusion | flops 15663104 | bytes 491776 | tf_op jit(solution)/shard_map/while/body/eval_jaxpr/reduce_sum | solution.py:220
  720.8 74.4 %reduce-scatter.2.cloned.1.call-done = f32[32,128]{1,0:T(8,128)} async-done(((f32[512,128]{1,0:T(8,128)}), f32[32,128]{1,0:T(8,128)}) %reduce-scatter.2.cloned.1.call-update) | async-done | bytes 16400 | tf_op jit(solution)/shard_map/reduce_scatter | solution.py:351
  (1906 shorter events, 505.7 us)
Async XLA Ops:
  12.4 624.5 %all-to-all-start.1 = ((s32[16,1,8]{2,1,0:T(1,128)}), s32[16,1,8]{2,1,0:T(1,128)}, u32[]{:S(2)}, u32[]{:S(2)}) async-start(s32[16,1,8]{2,1,0:T(1,128)} %bitcast.417), calls=%async_computation.1 | async-start | bytes 16384 | tf_op jit(solution)/shard_map/all_to_all | solution.py:337
  25.6 16.7 %collective-permute-start = (f32[10,1,1024]{2,1,0:T(1,128)S(1)}, f32[10,1,1024]{2,1,0:T(1,128)S(1)}, u32[]{:S(2)}, u32[]{:S(2)}) collective-permute-start(f32[10,1,1024]{2,1,0:T(1,128)S(1)} %get-tuple-element.752), channel_id=1, source_target_pairs={{0,1},{1,0},{2,3},{3,2},{4,5},{5,4},{6,7},{7,6},{8,9},{9,8},{10,11... | collective-permute-start | bytes 122888 | tf_op jit(solution)/shard_map/ppermute | solution.py:62
  25.7 15.7 %collective-permute-start.1 = (f32[10,1,1024]{2,1,0:T(1,128)S(1)}, f32[10,1,1024]{2,1,0:T(1,128)S(1)}, u32[]{:S(2)}, u32[]{:S(2)}) collective-permute-start(f32[10,1,1024]{2,1,0:T(1,128)S(1)} %get-tuple-element.753), channel_id=1, source_target_pairs={{1,0},{0,1},{3,2},{2,3},{5,4},{4,5},{7,6},{6,7},{9,8},{8,9},{11,10... | collective-permute-start | bytes 122888 | tf_op jit(solution)/shard_map/ppermute | solution.py:65
  91.8 18.2 %collective-permute-start.16 = (f32[1,2880]{1,0:T(1,128)S(1)}, f32[1,2880]{1,0:T(1,128)S(1)}, u32[]{:S(2)}, u32[]{:S(2)}) collective-permute-start(f32[1,2880]{1,0:T(1,128)S(1)} %get-tuple-element.898), channel_id=1, source_target_pairs={{0,30},{2,0},{4,2},{6,4},{8,6},{10,8},{12,10},{14,12},{16,14},{18,... | collective-permute-start | bytes 34568 | tf_op jit(solution)/shard_map/ppermute | solution.py:168
  97.4 16.7 %collective-permute-start.15 = (f32[1,2880]{1,0:T(1,128)S(1)}, f32[1,2880]{1,0:T(1,128)S(1)}, u32[]{:S(2)}, u32[]{:S(2)}) collective-permute-start(f32[1,2880]{1,0:T(1,128)S(1)} %get-tuple-element.899), channel_id=1, source_target_pairs={{0,28},{2,30},{4,0},{6,2},{8,4},{10,6},{12,8},{14,10},{16,12},{18,... | collective-permute-start | bytes 34568 | tf_op jit(solution)/shard_map/ppermute | solution.py:168
  97.9 16.3 %collective-permute-start.14 = (f32[1,2880]{1,0:T(1,128)S(1)}, f32[1,2880]{1,0:T(1,128)S(1)}, u32[]{:S(2)}, u32[]{:S(2)}) collective-permute-start(f32[1,2880]{1,0:T(1,128)S(1)} %get-tuple-element.900), channel_id=1, source_target_pairs={{0,26},{2,28},{4,30},{6,0},{8,2},{10,4},{12,6},{14,8},{16,10},{18,... | collective-permute-start | bytes 34568 | tf_op jit(solution)/shard_map/ppermute | solution.py:168
  98.4 17.2 %collective-permute-start.13 = (f32[1,2880]{1,0:T(1,128)S(1)}, f32[1,2880]{1,0:T(1,128)S(1)}, u32[]{:S(2)}, u32[]{:S(2)}) collective-permute-start(f32[1,2880]{1,0:T(1,128)S(1)} %get-tuple-element.901), channel_id=1, source_target_pairs={{0,24},{2,26},{4,28},{6,30},{8,0},{10,2},{12,4},{14,6},{16,8},{18,... | collective-permute-start | bytes 34568 | tf_op jit(solution)/shard_map/ppermute | solution.py:168
  99.0 19.5 %collective-permute-start.12 = (f32[1,2880]{1,0:T(1,128)S(1)}, f32[1,2880]{1,0:T(1,128)S(1)}, u32[]{:S(2)}, u32[]{:S(2)}) collective-permute-start(f32[1,2880]{1,0:T(1,128)S(1)} %get-tuple-element.902), channel_id=1, source_target_pairs={{0,22},{2,24},{4,26},{6,28},{8,30},{10,0},{12,2},{14,4},{16,6},{18... | collective-permute-start | bytes 34568 | tf_op jit(solution)/shard_map/ppermute | solution.py:168
  121.1 17.8 %collective-permute-start.6 = (f32[1,2880]{1,0:T(1,128)S(1)}, f32[1,2880]{1,0:T(1,128)S(1)}, u32[]{:S(2)}, u32[]{:S(2)}) collective-permute-start(f32[1,2880]{1,0:T(1,128)S(1)} %get-tuple-element.908), channel_id=1, source_target_pairs={{0,10},{2,12},{4,14},{6,16},{8,18},{10,20},{12,22},{14,24},{16,26}... | collective-permute-start | bytes 34568 | tf_op jit(solution)/shard_map/ppermute | solution.py:168
  121.6 17.2 %collective-permute-start.5 = (f32[1,2880]{1,0:T(1,128)S(1)}, f32[1,2880]{1,0:T(1,128)S(1)}, u32[]{:S(2)}, u32[]{:S(2)}) collective-permute-start(f32[1,2880]{1,0:T(1,128)S(1)} %get-tuple-element.909), channel_id=1, source_target_pairs={{0,8},{2,10},{4,12},{6,14},{8,16},{10,18},{12,20},{14,22},{16,24},... | collective-permute-start | bytes 34568 | tf_op jit(solution)/shard_map/ppermute | solution.py:168
  123.5 15.4 %collective-permute-start.4 = (f32[1,2880]{1,0:T(1,128)S(1)}, f32[1,2880]{1,0:T(1,128)S(1)}, u32[]{:S(2)}, u32[]{:S(2)}) collective-permute-start(f32[1,2880]{1,0:T(1,128)S(1)} %get-tuple-element.910), channel_id=1, source_target_pairs={{0,6},{2,8},{4,10},{6,12},{8,14},{10,16},{12,18},{14,20},{16,22},{... | collective-permute-start | bytes 34568 | tf_op jit(solution)/shard_map/ppermute | solution.py:168
  126.8 12.1 %collective-permute-start.3 = (f32[1,2880]{1,0:T(1,128)S(1)}, f32[1,2880]{1,0:T(1,128)S(1)}, u32[]{:S(2)}, u32[]{:S(2)}) collective-permute-start(f32[1,2880]{1,0:T(1,128)S(1)} %get-tuple-element.911), channel_id=1, source_target_pairs={{0,4},{2,6},{4,8},{6,10},{8,12},{10,14},{12,16},{14,18},{16,20},{1... | collective-permute-start | bytes 34568 | tf_op jit(solution)/shard_map/ppermute | solution.py:168
  254.4 18.9 %collective-permute-start.33 = (f32[1,2880]{1,0:T(1,128)S(1)}, f32[1,2880]{1,0:T(1,128)S(1)}, u32[]{:S(2)}, u32[]{:S(2)}) collective-permute-start(f32[1,2880]{1,0:T(1,128)S(1)} %get-tuple-element.882), channel_id=1, source_target_pairs={{0,30},{2,0},{4,2},{6,4},{8,6},{10,8},{12,10},{14,12},{16,14},{18,... | collective-permute-start | bytes 34568 | tf_op jit(solution)/shard_map/ppermute | solution.py:168
  260.1 17.0 %collective-permute-start.32 = (f32[1,2880]{1,0:T(1,128)S(1)}, f32[1,2880]{1,0:T(1,128)S(1)}, u32[]{:S(2)}, u32[]{:S(2)}) collective-permute-start(f32[1,2880]{1,0:T(1,128)S(1)} %get-tuple-element.883), channel_id=1, source_target_pairs={{0,28},{2,30},{4,0},{6,2},{8,4},{10,6},{12,8},{14,10},{16,12},{18,... | collective-permute-start | bytes 34568 | tf_op jit(solution)/shard_map/ppermute | solution.py:168
  260.9 16.7 %collective-permute-start.31 = (f32[1,2880]{1,0:T(1,128)S(1)}, f32[1,2880]{1,0:T(1,128)S(1)}, u32[]{:S(2)}, u32[]{:S(2)}) collective-permute-start(f32[1,2880]{1,0:T(1,128)S(1)} %get-tuple-element.884), channel_id=1, source_target_pairs={{0,26},{2,28},{4,30},{6,0},{8,2},{10,4},{12,6},{14,8},{16,10},{18,... | collective-permute-start | bytes 34568 | tf_op jit(solution)/shard_map/ppermute | solution.py:168
  261.0 17.6 %collective-permute-start.30 = (f32[1,2880]{1,0:T(1,128)S(1)}, f32[1,2880]{1,0:T(1,128)S(1)}, u32[]{:S(2)}, u32[]{:S(2)}) collective-permute-start(f32[1,2880]{1,0:T(1,128)S(1)} %get-tuple-element.885), channel_id=1, source_target_pairs={{0,24},{2,26},{4,28},{6,30},{8,0},{10,2},{12,4},{14,6},{16,8},{18,... | collective-permute-start | bytes 34568 | tf_op jit(solution)/shard_map/ppermute | solution.py:168
  263.1 19.3 %collective-permute-start.29 = (f32[1,2880]{1,0:T(1,128)S(1)}, f32[1,2880]{1,0:T(1,128)S(1)}, u32[]{:S(2)}, u32[]{:S(2)}) collective-permute-start(f32[1,2880]{1,0:T(1,128)S(1)} %get-tuple-element.886), channel_id=1, source_target_pairs={{0,22},{2,24},{4,26},{6,28},{8,30},{10,0},{12,2},{14,4},{16,6},{18... | collective-permute-start | bytes 34568 | tf_op jit(solution)/shard_map/ppermute | solution.py:168
  284.0 19.6 %collective-permute-start.23 = (f32[1,2880]{1,0:T(1,128)S(1)}, f32[1,2880]{1,0:T(1,128)S(1)}, u32[]{:S(2)}, u32[]{:S(2)}) collective-permute-start(f32[1,2880]{1,0:T(1,128)S(1)} %get-tuple-element.892), channel_id=1, source_target_pairs={{0,10},{2,12},{4,14},{6,16},{8,18},{10,20},{12,22},{14,24},{16,26}... | collective-permute-start | bytes 34568 | tf_op jit(solution)/shard_map/ppermute | solution.py:168
  285.6 18.0 %collective-permute-start.22 = (f32[1,2880]{1,0:T(1,128)S(1)}, f32[1,2880]{1,0:T(1,128)S(1)}, u32[]{:S(2)}, u32[]{:S(2)}) collective-permute-start(f32[1,2880]{1,0:T(1,128)S(1)} %get-tuple-element.893), channel_id=1, source_target_pairs={{0,8},{2,10},{4,12},{6,14},{8,16},{10,18},{12,20},{14,22},{16,24},... | collective-permute-start | bytes 34568 | tf_op jit(solution)/shard_map/ppermute | solution.py:168
  286.4 17.1 %collective-permute-start.21 = (f32[1,2880]{1,0:T(1,128)S(1)}, f32[1,2880]{1,0:T(1,128)S(1)}, u32[]{:S(2)}, u32[]{:S(2)}) collective-permute-start(f32[1,2880]{1,0:T(1,128)S(1)} %get-tuple-element.894), channel_id=1, source_target_pairs={{0,6},{2,8},{4,10},{6,12},{8,14},{10,16},{12,18},{14,20},{16,22},{... | collective-permute-start | bytes 34568 | tf_op jit(solution)/shard_map/ppermute | solution.py:168
  289.7 13.9 %collective-permute-start.20 = (f32[1,2880]{1,0:T(1,128)S(1)}, f32[1,2880]{1,0:T(1,128)S(1)}, u32[]{:S(2)}, u32[]{:S(2)}) collective-permute-start(f32[1,2880]{1,0:T(1,128)S(1)} %get-tuple-element.895), channel_id=1, source_target_pairs={{0,4},{2,6},{4,8},{6,10},{8,12},{10,14},{12,16},{14,18},{16,20},{1... | collective-permute-start | bytes 34568 | tf_op jit(solution)/shard_map/ppermute | solution.py:168
  292.3 11.3 %collective-permute-start.19 = (f32[1,2880]{1,0:T(1,128)S(1)}, f32[1,2880]{1,0:T(1,128)S(1)}, u32[]{:S(2)}, u32[]{:S(2)}) collective-permute-start(f32[1,2880]{1,0:T(1,128)S(1)} %get-tuple-element.896), channel_id=1, source_target_pairs={{0,2},{2,4},{4,6},{6,8},{8,10},{10,12},{12,14},{14,16},{16,18},{18... | collective-permute-start | bytes 34568 | tf_op jit(solution)/shard_map/ppermute | solution.py:168
  418.9 17.7 %collective-permute-start.50 = (f32[1,2880]{1,0:T(1,128)S(1)}, f32[1,2880]{1,0:T(1,128)S(1)}, u32[]{:S(2)}, u32[]{:S(2)}) collective-permute-start(f32[1,2880]{1,0:T(1,128)S(1)} %get-tuple-element.866), channel_id=1, source_target_pairs={{0,30},{2,0},{4,2},{6,4},{8,6},{10,8},{12,10},{14,12},{16,14},{18,... | collective-permute-start | bytes 34568 | tf_op jit(solution)/shard_map/ppermute | solution.py:168
  424.6 16.1 %collective-permute-start.49 = (f32[1,2880]{1,0:T(1,128)S(1)}, f32[1,2880]{1,0:T(1,128)S(1)}, u32[]{:S(2)}, u32[]{:S(2)}) collective-permute-start(f32[1,2880]{1,0:T(1,128)S(1)} %get-tuple-element.867), channel_id=1, source_target_pairs={{0,28},{2,30},{4,0},{6,2},{8,4},{10,6},{12,8},{14,10},{16,12},{18,... | collective-permute-start | bytes 34568 | tf_op jit(solution)/shard_map/ppermute | solution.py:168
  424.6 16.2 %collective-permute-start.48 = (f32[1,2880]{1,0:T(1,128)S(1)}, f32[1,2880]{1,0:T(1,128)S(1)}, u32[]{:S(2)}, u32[]{:S(2)}) collective-permute-start(f32[1,2880]{1,0:T(1,128)S(1)} %get-tuple-element.868), channel_id=1, source_target_pairs={{0,26},{2,28},{4,30},{6,0},{8,2},{10,4},{12,6},{14,8},{16,10},{18,... | collective-permute-start | bytes 34568 | tf_op jit(solution)/shard_map/ppermute | solution.py:168
  424.6 18.1 %collective-permute-start.47 = (f32[1,2880]{1,0:T(1,128)S(1)}, f32[1,2880]{1,0:T(1,128)S(1)}, u32[]{:S(2)}, u32[]{:S(2)}) collective-permute-start(f32[1,2880]{1,0:T(1,128)S(1)} %get-tuple-element.869), channel_id=1, source_target_pairs={{0,24},{2,26},{4,28},{6,30},{8,0},{10,2},{12,4},{14,6},{16,8},{18,... | collective-permute-start | bytes 34568 | tf_op jit(solution)/shard_map/ppermute | solution.py:168
  426.2 19.3 %collective-permute-start.46 = (f32[1,2880]{1,0:T(1,128)S(1)}, f32[1,2880]{1,0:T(1,128)S(1)}, u32[]{:S(2)}, u32[]{:S(2)}) collective-permute-start(f32[1,2880]{1,0:T(1,128)S(1)} %get-tuple-element.870), channel_id=1, source_target_pairs={{0,22},{2,24},{4,26},{6,28},{8,30},{10,0},{12,2},{14,4},{16,6},{18... | collective-permute-start | bytes 34568 | tf_op jit(solution)/shard_map/ppermute | solution.py:168
  447.6 18.8 %collective-permute-start.40 = (f32[1,2880]{1,0:T(1,128)S(1)}, f32[1,2880]{1,0:T(1,128)S(1)}, u32[]{:S(2)}, u32[]{:S(2)}) collective-permute-start(f32[1,2880]{1,0:T(1,128)S(1)} %get-tuple-element.876), channel_id=1, source_target_pairs={{0,10},{2,12},{4,14},{6,16},{8,18},{10,20},{12,22},{14,24},{16,26}... | collective-permute-start | bytes 34568 | tf_op jit(solution)/shard_map/ppermute | solution.py:168
  448.7 17.8 %collective-permute-start.39 = (f32[1,2880]{1,0:T(1,128)S(1)}, f32[1,2880]{1,0:T(1,128)S(1)}, u32[]{:S(2)}, u32[]{:S(2)}) collective-permute-start(f32[1,2880]{1,0:T(1,128)S(1)} %get-tuple-element.877), channel_id=1, source_target_pairs={{0,8},{2,10},{4,12},{6,14},{8,16},{10,18},{12,20},{14,22},{16,24},... | collective-permute-start | bytes 34568 | tf_op jit(solution)/shard_map/ppermute | solution.py:168
  450.1 16.4 %collective-permute-start.38 = (f32[1,2880]{1,0:T(1,128)S(1)}, f32[1,2880]{1,0:T(1,128)S(1)}, u32[]{:S(2)}, u32[]{:S(2)}) collective-permute-start(f32[1,2880]{1,0:T(1,128)S(1)} %get-tuple-element.878), channel_id=1, source_target_pairs={{0,6},{2,8},{4,10},{6,12},{8,14},{10,16},{12,18},{14,20},{16,22},{... | collective-permute-start | bytes 34568 | tf_op jit(solution)/shard_map/ppermute | solution.py:168
  453.3 13.2 %collective-permute-start.37 = (f32[1,2880]{1,0:T(1,128)S(1)}, f32[1,2880]{1,0:T(1,128)S(1)}, u32[]{:S(2)}, u32[]{:S(2)}) collective-permute-start(f32[1,2880]{1,0:T(1,128)S(1)} %get-tuple-element.879), channel_id=1, source_target_pairs={{0,4},{2,6},{4,8},{6,10},{8,12},{10,14},{12,16},{14,18},{16,20},{1... | collective-permute-start | bytes 34568 | tf_op jit(solution)/shard_map/ppermute | solution.py:168
  640.4 154.7 %reduce-scatter.2.cloned.1.call-start = ((), (), s32[]{:S(2)}) async-start(), calls=%async_computation.3 | async-start | bytes 278528 | tf_op jit(solution)/shard_map/reduce_scatter | solution.py:351
  (457 other events, 3796.6 us)
Sparse Core Ops, SparseCore 0:
  720.9 74.1 reduce-scatter.1
